TPU v7x, 256 devices: a whole 4x4x8 slice. The times are simulated.
256 devices in a mesh: ep: 32 (over x, z), tp: 8 (over y, core).
Axes of the slice: x: 4, y: 4, z: 8, core: 2. Of those that a mesh axis runs over, the one named last changes fastest.
Arguments:
- tokens: bfloat16 [8192, 2880], P('ep', 'tp'), may hold values from -6 to 6
- expert_ids: int32 [8192, 4], P('ep'), may hold values from 0 to 63, all different within a row; in each aligned block of 256 rows (0 to 255, 256 to 511, ...) at most 32 rows name the same one
- combine_weights: float32 [8192, 4], P('ep'), may hold values from 0.05 to 0.6
- gate_weight: bfloat16 [64, 2880, 2880], P('ep', None, 'tp'), may hold values from -0.109375 to 0.109375
- up_weight: bfloat16 [64, 2880, 2880], P('ep', None, 'tp'), may hold values from -0.109375 to 0.109375
- down_weight: bfloat16 [64, 2880, 2880], P('ep', 'tp'), may hold values from -0.109375 to 0.109375
Outputs:
- mixed: bfloat16 [8192, 2880], P('ep', 'tp')
Inputs may be any that keep to these rules, and one draw needn't show every extreme that they name: `expert_ids`: each row names 4 different experts; within the 256 rows of one index of ep no expert is named more than 32 times, a bound that some block reaches.
All inputs are finite; a program needn't handle non-finite values.
Results may differ from a plain program's by a relative error of at most 0.014.
Values may be sent and summed in bfloat16 or wider, within the bound.
No kernel may reach another device: no remote copies, remote signals or barrier semaphores. Data moves between devices by JAX's collectives and lax.ppermute only.
A program may use at most 128 MiB of HBM per device.

v0:
```python
import jax
import jax.numpy as jnp
from jax import lax
from jax.sharding import Mesh
from jax.sharding import PartitionSpec as P

TP = ("tp_0", "tp_1")


def reduced_to_own(pieces, axes, sequence):
    inside = pieces.shape[1:]
    pieces = pieces.reshape(*(lax.axis_size(a) for a in axes), *inside)
    pieces = jnp.moveaxis(pieces, sequence, range(len(axes))).reshape(-1, *inside)
    for k in sequence:
        pieces = lax.psum_scatter(pieces, axes[k], scatter_dimension=0, tiled=True)
    return pieces[0]


def split_up(array, dim, count):
    before, after = (array.shape[:dim], array.shape[dim + 1 :])
    return jnp.moveaxis(array.reshape(*before, count, -1, *after), dim, 0)


def scatter_axes(array, axes, sequence, dim):
    count = lax.axis_size(axes)
    return reduced_to_own(split_up(array, dim, count), axes, sequence)


def activate(gate_acc, up_acc):
    return (up_acc + 1.0) * gate_acc * jax.nn.sigmoid(1.702 * gate_acc)


def local(tokens, expert_ids, combine_weights, gate_weight, up_weight, down_weight):
    ep_count = lax.axis_size("ep")
    exp_local = gate_weight.shape[0]
    experts = exp_local * ep_count
    tok_rows = expert_ids.shape[0]
    top_count = expert_ids.shape[1]
    capacity = 2 * tok_rows * top_count // experts
    feat_width = tokens.shape[1]
    flat_ids = expert_ids.reshape(-1)
    onehot = (flat_ids[:, None] == jnp.arange(experts, dtype=jnp.int32)[None, :]).astype(jnp.int32)
    slot_pos = jnp.sum((jnp.cumsum(onehot, axis=0) - onehot) * onehot, axis=1)
    expert_local = flat_ids % exp_local
    owner_dev = flat_ids // exp_local
    token_of = jnp.arange(tok_rows * top_count, dtype=jnp.int32) // top_count
    send_buf = jnp.zeros((exp_local, ep_count, capacity, feat_width), jnp.bfloat16)
    send_buf = send_buf.at[expert_local, owner_dev, slot_pos].set(tokens[token_of])
    arrived = lax.all_to_all(send_buf, "ep", split_axis=1, concat_axis=1, tiled=True)
    arrived = arrived.reshape(exp_local, ep_count * capacity, feat_width)
    shard_piece = lax.all_gather(arrived, TP, axis=2, tiled=True)
    gate_new = jnp.einsum(
        "erd,edf->erf", shard_piece, gate_weight, preferred_element_type=jnp.float32
    )
    up_new = jnp.einsum("erd,edf->erf", shard_piece, up_weight, preferred_element_type=jnp.float32)
    hidden = activate(gate_new, up_new).astype(jnp.bfloat16)
    partials = jnp.einsum("erf,efd->erd", hidden, down_weight, preferred_element_type=jnp.float32)
    weights_flat = combine_weights.reshape(-1)
    summed = scatter_axes(partials.astype(jnp.bfloat16), TP, (1, 0), 2).astype(jnp.float32)
    summed = summed.reshape(exp_local, ep_count, capacity, summed.shape[2])
    returned = lax.all_to_all(
        summed.astype(jnp.bfloat16), "ep", split_axis=1, concat_axis=1, tiled=True
    ).astype(summed.dtype)
    picked = returned[expert_local, owner_dev, slot_pos]
    weighted = (picked * weights_flat[:, None]).reshape(tok_rows, top_count, picked.shape[1])
    mixed = jnp.sum(weighted, axis=1).astype(jnp.bfloat16)
    return mixed


def solution(mesh):
    split = Mesh(mesh.devices.reshape(mesh.shape["ep"], 4, 2), ("ep", "tp_0", "tp_1"))
    placed = (
        P("ep", TP),
        P("ep", None),
        P("ep", None),
        P("ep", None, TP),
        P("ep", None, TP),
        P("ep", TP, None),
    )
    return jax.shard_map(local, mesh=split, in_specs=placed, out_specs=P("ep", TP), check_vma=False)
```

profile of v0, /device:TPU:32, one launch (start us, length us, event | category | flops | bytes accessed | tf_op | source)
XLA Modules:
  0.0 360.9 jit_solution(3638396333141942187)
XLA Ops:
  6.5 0.0 copy-start.3
  6.5 0.0 copy-start.2
  6.5 0.0 all-gather.2.cloned.1.call-start
  6.5 0.9 copy.61
  7.4 0.1 eq.31
  7.5 0.1 eq.27
  7.6 0.1 reshape.218
  7.8 18.0 %reduce-window.6 = s32[64,8,128]{2,1,0:T(8,128)S(1)} reduce-window(s32[64,8,128]{2,1,0:T(8,128)S(1)} %fusion.6, s32[]{:T(128)} %constant.47.clone.1), window={size=1x1x128 pad=0_0x0_0x127_0}, to_apply=%region_0.0 | reduce-window | flops 8323072 | bytes 524292 | tf_op jit(solution)/shard_map/reduce-window
  25.8 0.1 slice.13
  26.0 0.1 copy.64
  26.1 0.1 copy.65
  26.2 0.1 broadcast_add_fusion
  26.4 0.1 fusion.5
  26.4 0.1 shift-left_or_fusion
  26.5 0.0 copy-done.3
  26.5 0.1 multiply_reduce_fusion.1
  26.6 0.0 copy-done.2
  26.6 0.1 and_reduce_fusion
  26.7 0.0 copy-done
  26.7 0.2 copy.66
  26.9 9.4 %scatter_custom_fusion = bf16[2048,360]{1,0:T(8,128)(2,1)S(1)} fusion(s32[1024]{0:T(1024)S(1)} %get-tuple-element.10, bf16[256,360]{1,0:T(8,128)(2,1)S(1)} %copy.66, s32[1024]{0:T(1024)S(1)} %get-tuple-element.9, bf16[]{:T(256)} %constant.46.clone.1), kind=kCustom, calls=%fused_computation.7 | custom fusion | bytes 1474562
  36.3 0.3 copy.67
  36.6 51.1 %all_to_all.10 = bf16[2,32,32,360]{3,2,0,1:T(8,128)(2,1)S(1)} all-to-all(bf16[2,32,32,360]{3,2,0,1:T(8,128)(2,1)S(1)} %copy.67), channel_id=1, replica_groups=mesh['ep'=32,'tp_0'=4,'tp_1'=2] {'ep'}, dimensions={1} | all-to-all | bytes 2949120 | tf_op jit(solution)/shard_map/all_to_all | solution.py:49
  87.6 0.2 copy.68
  87.8 1.6 copy.69
  89.4 0.0 all-gather.2.cloned.1.call-update
  89.5 0.2 reduce-scatter.3.cloned.1.call-start
  89.7 62.7 %all-gather.2.cloned.1.call-done = bf16[2,1024,2880]{1,2,0:T(8,128)(2,1)} async-done(((bf16[2,1024,360]{1,2,0:T(8,128)(2,1)}), bf16[2,1024,2880]{1,2,0:T(8,128)(2,1)}) %all-gather.2.cloned.1.call-update) | async-done | bytes 11796496 | tf_op jit(solution)/shard_map/all_gather | solution.py:51
  152.4 8.8 %fusion.7 = f32[2,1024,360]{1,2,0:T(8,128)S(1)} fusion(bf16[2,1024,2880]{1,2,0:T(8,128)(2,1)} %all-gather.2.cloned.1.call-done, bf16[2,2880,360]{1,2,0:T(8,128)(2,1)} %param.9), kind=kOutput, calls=%fused_computation.37 | convolution fusion | flops 4246732800 | bytes 18892800 | tf_op jit(solution)/shard_map/erd,edf->erf/dot_general | solution.py:52
  161.3 18.4 %convolution_convert_fusion = bf16[2,1024,2880]{1,2,0:T(8,128)(2,1)} fusion(bf16[2,360,2880]{2,1,0:T(8,128)(2,1)} %param.11, f32[2,1024,360]{1,2,0:T(8,128)S(1)} %fusion.7, bf16[2,1024,2880]{1,2,0:T(8,128)(2,1)} %all-gather.2.cloned.1.call-done, bf16[2,2880,360]{1,2,0:T(8,128)(2,1)} %param.10), kind=kOutput, calls=%fused_computation.3 | convolution fusion | flops 8505262080 | bytes 34836480 | tf_op jit(solution)/shard_map/erf,efd->erd/dot_general | solution.py:57
  179.7 10.2 %copy.71 = bf16[2,4,2,1024,360]{3,4,2,1,0:T(8,128)(2,1)} copy(bf16[2,4,2,1024,360]{3,4,0,1,2:T(8,128)(2,1)} %bitcast.47) | data formatting | bytes 23592960 | tf_op jit(solution)/shard_map/transpose | solution.py:13
  189.9 0.0 reduce-scatter.3.cloned.1.call-update
  190.0 0.0 reduce-scatter.5.cloned.1.call-start
  190.0 26.8 %reduce-scatter.3.cloned.1.call-done = bf16[4,2,1024,360]{2,3,1,0:T(8,128)(2,1)} async-done(((bf16[8,2,1024,360]{2,3,1,0:T(8,128)(2,1)}), bf16[4,2,1024,360]{2,3,1,0:T(8,128)(2,1)}) %reduce-scatter.3.cloned.1.call-update) | async-done | bytes 5898256 | tf_op jit(solution)/shard_map/reduce_scatter | solution.py:15
  216.8 0.0 reduce-scatter.5.cloned.1.call-update
  216.8 65.4 %reduce-scatter.5.cloned.1.call-done = bf16[1,2,1024,360]{2,3,1,0:T(8,128)(2,1)} async-done(((bf16[4,2,1024,360]{2,3,1,0:T(8,128)(2,1)}), bf16[1,2,1024,360]{2,3,1,0:T(8,128)(2,1)}) %reduce-scatter.5.cloned.1.call-update) | async-done | bytes 1474576 | tf_op jit(solution)/shard_map/reduce_scatter | solution.py:15
  282.2 1.8 copy.72
  284.1 0.0 copy-start.1
  284.1 1.4 copy.73
  285.5 10.1 %all-to-all-start.1 = ((bf16[2,32,32,360]{3,2,0,1:T(8,128)(2,1)}), bf16[2,32,32,360]{3,2,0,1:T(8,128)(2,1)}, u32[]{:S(2)}, u32[]{:S(2)}) async-start(bf16[2,32,32,360]{3,2,0,1:T(8,128)(2,1)} %copy.73), calls=%async_computation.3 | async-start | bytes 3145728 | tf_op jit(solution)/shard_map/all_to_all | solution.py:61
  295.6 0.0 copy-done.1
  295.6 0.1 copy.75
  295.8 39.0 %all-to-all-done.1 = bf16[2,32,32,360]{3,2,0,1:T(8,128)(2,1)} async-done(((bf16[2,32,32,360]{3,2,0,1:T(8,128)(2,1)}), bf16[2,32,32,360]{3,2,0,1:T(8,128)(2,1)}, u32[]{:S(2)}, u32[]{:S(2)}) %all-to-all-start.1) | async-done | bytes 1474592 | tf_op jit(solution)/shard_map/all_to_all | solution.py:61
  334.8 1.8 copy_convert_fusion
  336.6 14.1 %gather_fusion = f32[1024,360]{1,0:T(8,128)} fusion(f32[2,32,32,360]{3,2,1,0:T(8,128)S(1)} %copy_convert_fusion, s32[1024]{0:T(1024)S(1)} %bitcast.45), kind=kCustom, calls=%fused_computation.1 | custom fusion | bytes 2961408 | tf_op jit(solution)/shard_map/gather | solution.py:64
  350.7 1.8 gather.10
  352.5 1.0 multiply_reduce_fusion
  353.5 0.8 copy.76
  (6 shorter events, 0.1 us)
Async XLA Ops:
  6.5 20.0 %copy-start.3 = (s32[3]{0:T(128)S(1)}, s32[3]{0:T(128)}, u32[]{:S(2)}) copy-start(s32[3]{0:T(128)} %constant.60) | copy-start | bytes 40
  6.5 20.1 %copy-start.2 = (s32[3]{0:T(128)S(1)}, s32[3]{0:T(128)}, u32[]{:S(2)}) copy-start(s32[3]{0:T(128)} %constant.63) | copy-start | bytes 40
  6.5 20.2 %copy-start = (bf16[256,360]{0,1:T(8,128)(2,1)S(1)}, bf16[256,360]{0,1:T(8,128)(2,1)}, u32[]{:S(2)}) copy-start(bf16[256,360]{0,1:T(8,128)(2,1)} %param.6) | copy-start | bytes 552964
  6.5 145.9 %all-gather.2.cloned.1.call-start = ((), (), s32[]{:S(2)}) async-start(), calls=%async_computation.4 | async-start | bytes 13271040 | tf_op jit(solution)/shard_map/all_gather | solution.py:51
  89.5 127.3 %reduce-scatter.3.cloned.1.call-start = ((), (), s32[]{:S(2)}) async-start(), calls=%async_computation.5 | async-start | bytes 17694720 | tf_op jit(solution)/shard_map/reduce_scatter | solution.py:15
  190.0 92.3 %reduce-scatter.5.cloned.1.call-start = ((), (), s32[]{:S(2)}) async-start(), calls=%async_computation.6 | async-start | bytes 7372800 | tf_op jit(solution)/shard_map/reduce_scatter | solution.py:15
  284.1 11.5 %copy-start.1 = (f32[256,4]{0,1:T(4,128)S(1)}, f32[256,4]{0,1:T(4,128)}, u32[]{:S(2)}) copy-start(f32[256,4]{0,1:T(4,128)} %param.8) | copy-start | bytes 12292
  285.5 49.3 %all-to-all-start.1 = ((bf16[2,32,32,360]{3,2,0,1:T(8,128)(2,1)}), bf16[2,32,32,360]{3,2,0,1:T(8,128)(2,1)}, u32[]{:S(2)}, u32[]{:S(2)}) async-start(bf16[2,32,32,360]{3,2,0,1:T(8,128)(2,1)} %copy.73), calls=%async_computation.3 | async-start | bytes 3145728 | tf_op jit(solution)/shard_map/all_to_all | solution.py:61
Sparse Core Ops, SparseCore 0:
  89.6 62.7 all-gather.1
  190.1 26.6 reduce-scatter.2
  219.4 62.7 reduce-scatter.4
where the time goes:
time: 361 us
  waiting for transfers between devices  194 us (54%)
  blocking collectives  51.1 us (14%)
  local copies, waits for them, and re-layouts  43.5 us (12%)
  matrix products  27.3 us (8%)
  other arithmetic  21.4 us (6%)
  between operations  13.3 us (4%)
  starting transfers between devices  10.4 us (3%)
    reduce_scatter x2, waiting for transfers between devices, reduced_to_own(): pieces = lax.psum_scatter(pieces, axes[k], scatter_dimension=0, tiled=True)  92.2 us
    all_gather x1, waiting for transfers between devices, local(): shard_piece = lax.all_gather(arrived, TP, axis=2, tiled=True)  62.7 us
    all_to_all x1, blocking collectives, local(): lax.all_to_all(send_buf, 'ep', split_axis=1, concat_axis=1, tiled=True)  51.1 us
    all_to_all x1, waiting for transfers between devices, local(): lax.all_to_all(summed.astype(jnp.bfloat16), 'ep', split_axis=1, concat_ax...  39 us
    dot_general x1, matrix products, local(): jnp.einsum('erf,efd->erd', hidden, down_weight, preferred_element_type=jn...  18.4 us
    another operation x3, other arithmetic  18.2 us
    gather x2, local copies, waits for them, and re-layouts, local(): picked = returned[expert_local, owner_dev, slot_pos]  15.9 us
    unnamed x12, local copies, waits for them, and re-layouts  10.5 us
  transfers between devices with their start and end apart: 4, of which 4 were waited for; matrix products, arithmetic and copies ran while one was open for 0% of the time, Pallas kernels for 0%

commit v1 on v0

--- a/solution.py
+++ b/solution.py
@@ -1,3 +1,4 @@
+import functools
 import jax
 import jax.numpy as jnp
 from jax import lax
@@ -5,6 +6,20 @@
 from jax.sharding import PartitionSpec as P
 
 TP = ("tp_0", "tp_1")
+
+
+def sample_map(z_in, lane_axis, dim_no):
+    leaves = []
+    for _ in range(lax.axis_size(lane_axis)):
+        leaves.append(z_in)
+    arr_out = jnp.concatenate(
+        lax.all_to_all(jnp.stack(leaves, axis=0), axis_name=lane_axis, split_axis=0, concat_axis=0),
+        axis=dim_no,
+    )
+    return arr_out
+
+
+slots_lift = functools.partial(sample_map, lane_axis=TP, dim_no=2)
 
 
 def reduced_to_own(pieces, axes, sequence):
@@ -48,7 +63,7 @@
     send_buf = send_buf.at[expert_local, owner_dev, slot_pos].set(tokens[token_of])
     arrived = lax.all_to_all(send_buf, "ep", split_axis=1, concat_axis=1, tiled=True)
     arrived = arrived.reshape(exp_local, ep_count * capacity, feat_width)
-    shard_piece = lax.all_gather(arrived, TP, axis=2, tiled=True)
+    shard_piece = slots_lift(arrived)
     gate_new = jnp.einsum(
         "erd,edf->erf", shard_piece, gate_weight, preferred_element_type=jnp.float32
     )

time: 361 us -> 441 us (1.22)
  blocking collectives: 51.1 us -> 187 us
  waiting for transfers between devices: 194 us -> 128 us
  local copies, waits for them, and re-layouts: 43.5 us -> 53.8 us
    all_to_all x0 -> x1, blocking collectives: none -> 136 us  [sample_map(): lax.all_to_all(jnp.stack(leaves, axis=0), axis_name=lane_axis, split_axis...]
    all_gather x1 -> x0, waiting for transfers between devices: 62.7 us -> none  [local(): shard_piece = lax.all_gather(arrived, TP, axis=2, tiled=True)]
    another operation x2 -> x4, local copies, waits for them, and re-layouts: 0.09 us -> 6.79 us  [the longest x2 6.7 us: sample_map(): jnp.stack(leaves, axis=0)]
  transfers between devices with their start and end apart: 4 -> 3, of which waited for: 4 -> 3; matrix products, arithmetic and copies ran while one was open for 0% -> 0% of each run, Pallas kernels for 0% -> 0%
where the time goes in v1:
time: 441 us
  blocking collectives  187 us (42%)
  waiting for transfers between devices  128 us (29%)
  local copies, waits for them, and re-layouts  53.8 us (12%)
  matrix products  27.3 us (6%)
  other arithmetic  21.4 us (5%)
  between operations  13.6 us (3%)
  starting transfers between devices  10.1 us (2%)
    all_to_all x1, blocking collectives, sample_map(): lax.all_to_all(jnp.stack(leaves, axis=0), axis_name=lane_axis, split_axis...  136 us
    reduce_scatter x2, waiting for transfers between devices, reduced_to_own(): pieces = lax.psum_scatter(pieces, axes[k], scatter_dimension=0, tiled=True)  89 us
    all_to_all x1, blocking collectives, local(): lax.all_to_all(send_buf, 'ep', split_axis=1, concat_axis=1, tiled=True)  51.1 us
    all_to_all x1, waiting for transfers between devices, local(): lax.all_to_all(summed.astype(jnp.bfloat16), 'ep', split_axis=1, concat_ax...  39 us
    dot_general x1, matrix products, local(): jnp.einsum('erf,efd->erd', hidden, down_weight, preferred_element_type=jn...  18.4 us
    another operation x3, other arithmetic  18.2 us
    gather x2, local copies, waits for them, and re-layouts, local(): picked = returned[expert_local, owner_dev, slot_pos]  15.9 us
    unnamed x12, local copies, waits for them, and re-layouts  10.5 us
  transfers between devices with their start and end apart: 3, of which 3 were waited for; matrix products, arithmetic and copies ran while one was open for 0% of the time, Pallas kernels for 0%

profile of v1, /device:TPU:32, one launch (start us, length us, event | category | flops | bytes accessed | tf_op | source)
XLA Modules:
  0.0 440.8 jit_solution(7967100099624271598)
XLA Ops:
  6.5 0.0 copy-start.3
  6.5 0.0 copy-start.2
  6.5 0.0 reduce-scatter.3.cloned.1.call-start
  6.5 0.9 copy.64
  7.4 0.1 eq.31
  7.5 0.1 eq.27
  7.6 0.1 reshape.223
  7.8 18.0 %reduce-window.6 = s32[64,8,128]{2,1,0:T(8,128)S(1)} reduce-window(s32[64,8,128]{2,1,0:T(8,128)S(1)} %fusion.6, s32[]{:T(128)} %constant.47.clone.1), window={size=1x1x128 pad=0_0x0_0x127_0}, to_apply=%region_0.0 | reduce-window | flops 8323072 | bytes 524292 | tf_op jit(solution)/shard_map/reduce-window
  25.8 0.1 slice.13
  26.0 0.1 copy.67
  26.1 0.1 copy.68
  26.2 0.1 broadcast_add_fusion
  26.4 0.1 fusion.5
  26.4 0.1 shift-left_or_fusion
  26.5 0.0 copy-done.3
  26.5 0.1 multiply_reduce_fusion.1
  26.6 0.0 copy-done.2
  26.6 0.1 and_reduce_fusion
  26.7 0.0 copy-done
  26.7 0.2 copy.69
  26.9 9.4 %scatter_custom_fusion = bf16[2048,360]{1,0:T(8,128)(2,1)S(1)} fusion(s32[1024]{0:T(1024)S(1)} %get-tuple-element.10, bf16[256,360]{1,0:T(8,128)(2,1)S(1)} %copy.69, s32[1024]{0:T(1024)S(1)} %get-tuple-element.9, bf16[]{:T(256)} %constant.46.clone.1), kind=kCustom, calls=%fused_computation.7 | custom fusion | bytes 1474562
  36.3 0.3 copy.70
  36.6 51.1 %all_to_all.15 = bf16[2,32,32,360]{3,2,0,1:T(8,128)(2,1)S(1)} all-to-all(bf16[2,32,32,360]{3,2,0,1:T(8,128)(2,1)S(1)} %copy.70), channel_id=1, replica_groups=mesh['ep'=32,'tp_0'=4,'tp_1'=2] {'ep'}, dimensions={1} | all-to-all | bytes 2949120 | tf_op jit(solution)/shard_map/all_to_all | solution.py:64
  87.6 0.2 copy.71
  87.8 0.7 copy.72
  88.6 6.0 %stack.3 = bf16[8,2,1024,360]{2,3,1,0:T(8,128)(2,1)} broadcast(bf16[2,1024,360]{1,2,0:T(8,128)(2,1)S(1)} %copy.72), dimensions={1,2,3} | broadcast | bytes 13271040 | tf_op jit(solution)/shard_map/stack | solution.py:16
  94.5 135.6 %all_to_all.16 = bf16[8,2,1024,360]{2,3,1,0:T(8,128)(2,1)S(1)} all-to-all(bf16[8,2,1024,360]{2,3,1,0:T(8,128)(2,1)} %stack.3), channel_id=1, replica_groups=mesh['ep'=32,'tp_0'=4,'tp_1'=2] {'tp_0','tp_1'}, dimensions={0} | all-to-all | bytes 23592960 | tf_op jit(solution)/shard_map/all_to_all | solution.py:16
  230.1 5.1 %copy.73 = bf16[2,1024,8,360]{1,3,2,0:T(8,128)(2,1)} copy(bf16[2,1024,8,360]{1,3,0,2:T(8,128)(2,1)S(1)} %bitcast.49) | data formatting | bytes 23592960 | tf_op jit(solution)/shard_map/reshape | solution.py:15
  235.2 8.8 %fusion.7 = f32[2,1024,360]{1,2,0:T(8,128)S(1)} fusion(bf16[2,1024,2880]{1,2,0:T(8,128)(2,1)} %bitcast.50, bf16[2,2880,360]{1,2,0:T(8,128)(2,1)} %param.9), kind=kOutput, calls=%fused_computation.37 | convolution fusion | flops 4246732800 | bytes 18892800 | tf_op jit(solution)/shard_map/erd,edf->erf/dot_general | solution.py:67
  244.1 18.4 %convolution_convert_fusion = bf16[2,1024,2880]{1,2,0:T(8,128)(2,1)} fusion(bf16[2,360,2880]{2,1,0:T(8,128)(2,1)} %param.11, f32[2,1024,360]{1,2,0:T(8,128)S(1)} %fusion.7, bf16[2,1024,2880]{1,2,0:T(8,128)(2,1)} %bitcast.51, bf16[2,2880,360]{1,2,0:T(8,128)(2,1)} %param.10), kind=kOutput, calls=%fused_computation.3 | convolution fusion | flops 8505262080 | bytes 34836480 | tf_op jit(solution)/shard_map/erf,efd->erd/dot_general | solution.py:72
  262.5 10.2 %copy.75 = bf16[2,4,2,1024,360]{3,4,2,1,0:T(8,128)(2,1)} copy(bf16[2,4,2,1024,360]{3,4,0,1,2:T(8,128)(2,1)} %bitcast.52) | data formatting | bytes 23592960 | tf_op jit(solution)/shard_map/transpose | solution.py:28
  272.8 0.0 reduce-scatter.3.cloned.1.call-update
  272.8 0.0 reduce-scatter.5.cloned.1.call-start
  272.8 19.8 %reduce-scatter.3.cloned.1.call-done = bf16[4,2,1024,360]{2,3,1,0:T(8,128)(2,1)} async-done(((bf16[8,2,1024,360]{2,3,1,0:T(8,128)(2,1)}), bf16[4,2,1024,360]{2,3,1,0:T(8,128)(2,1)}) %reduce-scatter.3.cloned.1.call-update) | async-done | bytes 5898256 | tf_op jit(solution)/shard_map/reduce_scatter | solution.py:30
  292.7 0.0 reduce-scatter.5.cloned.1.call-update
  292.7 69.1 %reduce-scatter.5.cloned.1.call-done = bf16[1,2,1024,360]{2,3,1,0:T(8,128)(2,1)} async-done(((bf16[4,2,1024,360]{2,3,1,0:T(8,128)(2,1)}), bf16[1,2,1024,360]{2,3,1,0:T(8,128)(2,1)}) %reduce-scatter.5.cloned.1.call-update) | async-done | bytes 1474576 | tf_op jit(solution)/shard_map/reduce_scatter | solution.py:30
  361.8 1.9 copy.76
  363.7 0.0 copy-start.1
  363.7 1.5 copy.77
  365.2 10.1 %all-to-all-start.2 = ((bf16[2,32,32,360]{3,2,0,1:T(8,128)(2,1)}), bf16[2,32,32,360]{3,2,0,1:T(8,128)(2,1)}, u32[]{:S(2)}, u32[]{:S(2)}) async-start(bf16[2,32,32,360]{3,2,0,1:T(8,128)(2,1)} %copy.77), calls=%async_computation.4 | async-start | bytes 3145728 | tf_op jit(solution)/shard_map/all_to_all | solution.py:76
  375.2 0.0 copy-done.1
  375.3 0.1 copy.79
  375.4 39.0 %all-to-all-done.2 = bf16[2,32,32,360]{3,2,0,1:T(8,128)(2,1)} async-done(((bf16[2,32,32,360]{3,2,0,1:T(8,128)(2,1)}), bf16[2,32,32,360]{3,2,0,1:T(8,128)(2,1)}, u32[]{:S(2)}, u32[]{:S(2)}) %all-to-all-start.2) | async-done | bytes 1474592 | tf_op jit(solution)/shard_map/all_to_all | solution.py:76
  414.4 1.8 copy_convert_fusion
  416.2 14.1 %gather_fusion = f32[1024,360]{1,0:T(8,128)} fusion(f32[2,32,32,360]{3,2,1,0:T(8,128)S(1)} %copy_convert_fusion, s32[1024]{0:T(1024)S(1)} %bitcast.47), kind=kCustom, calls=%fused_computation.1 | custom fusion | bytes 2961408 | tf_op jit(solution)/shard_map/gather | solution.py:79
  430.4 1.8 gather.10
  432.1 1.0 multiply_reduce_fusion
  433.2 0.8 copy.80
  (6 shorter events, 0.1 us)
Async XLA Ops:
  6.5 20.0 %copy-start.3 = (s32[3]{0:T(128)S(1)}, s32[3]{0:T(128)}, u32[]{:S(2)}) copy-start(s32[3]{0:T(128)} %constant.60) | copy-start | bytes 40
  6.5 20.1 %copy-start.2 = (s32[3]{0:T(128)S(1)}, s32[3]{0:T(128)}, u32[]{:S(2)}) copy-start(s32[3]{0:T(128)} %constant.63) | copy-start | bytes 40
  6.5 20.2 %copy-start = (bf16[256,360]{0,1:T(8,128)(2,1)S(1)}, bf16[256,360]{0,1:T(8,128)(2,1)}, u32[]{:S(2)}) copy-start(bf16[256,360]{0,1:T(8,128)(2,1)} %param.6) | copy-start | bytes 552964
  6.5 286.1 %reduce-scatter.3.cloned.1.call-start = ((), (), s32[]{:S(2)}) async-start(), calls=%async_computation.5 | async-start | bytes 17694720 | tf_op jit(solution)/shard_map/reduce_scatter | solution.py:30
  272.8 89.0 %reduce-scatter.5.cloned.1.call-start = ((), (), s32[]{:S(2)}) async-start(), calls=%async_computation.6 | async-start | bytes 7372800 | tf_op jit(solution)/shard_map/reduce_scatter | solution.py:30
  363.7 11.6 %copy-start.1 = (f32[256,4]{0,1:T(4,128)S(1)}, f32[256,4]{0,1:T(4,128)}, u32[]{:S(2)}) copy-start(f32[256,4]{0,1:T(4,128)} %param.8) | copy-start | bytes 12292
  365.2 49.2 %all-to-all-start.2 = ((bf16[2,32,32,360]{3,2,0,1:T(8,128)(2,1)}), bf16[2,32,32,360]{3,2,0,1:T(8,128)(2,1)}, u32[]{:S(2)}, u32[]{:S(2)}) async-start(bf16[2,32,32,360]{3,2,0,1:T(8,128)(2,1)} %copy.77), calls=%async_computation.4 | async-start | bytes 3145728 | tf_op jit(solution)/shard_map/all_to_all | solution.py:76
Sparse Core Ops, SparseCore 0:
  272.9 19.7 reduce-scatter.2
  295.2 66.5 reduce-scatter.4
